TPU v7x, 16 devices: a whole 2x2x2 slice. The times are simulated.
16 devices in a mesh: tp: 4 (over z, y), dp: 4 (over x, core).
Axes of the slice: x: 2, y: 2, z: 2, core: 2. Of those that a mesh axis runs over, the one named last changes fastest.
Arguments:
- hidden: bfloat16 [8192, 2048], P('dp')
- labels: int32 [8192], P('dp')
- loss_mask: int32 [8192], P('dp')
- norm_gain: bfloat16 [2048], replicated
- w_out: bfloat16 [2048, 32000], P(None, 'tp')
Outputs:
- output 1: float32 [], replicated
- output 2: bfloat16 [8192, 2048], P('dp')
- output 3: float32 [2048, 32000], P(None, 'tp')
- output 4: float32 [2048], replicated
All inputs are finite; a program needn't handle non-finite values.
Results may differ from a plain program's by a relative error of at most 0.001.
Values sent between devices are 32-bit elements.
A program may use at most 1 GiB of HBM per device.

v0:
```python
import jax
import jax.numpy as jnp
from jax import lax
from jax.sharding import PartitionSpec as P

NORM_EPS = 1e-5


def solution(mesh):
    def local_head(hidden, labels, loss_mask, norm_gain, w_out):
        vocab_local = w_out.shape[1]
        vocab_start = lax.axis_index("tp") * vocab_local
        mask_f = loss_mask.astype(jnp.float32)
        mask_total = lax.psum(jnp.sum(mask_f), "dp")
        gain_f = norm_gain.astype(jnp.float32)
        h_f32 = hidden.astype(jnp.float32)
        r_inv = lax.rsqrt(jnp.mean(h_f32 * h_f32, axis=-1, keepdims=True) + NORM_EPS)
        x_hat = h_f32 * r_inv
        normed = (x_hat * gain_f).astype(jnp.bfloat16)
        logits = jnp.dot(normed, w_out, preferred_element_type=jnp.float32)
        row_max = lax.pmax(jnp.max(logits, axis=-1, keepdims=True), "tp")
        shifted = jnp.exp(logits - row_max)
        sum_exp = lax.psum(jnp.sum(shifted, axis=-1, keepdims=True), "tp")
        is_label = lax.broadcasted_iota(jnp.int32, (1, vocab_local), 1) == (labels - vocab_start)[:, None]
        target = lax.psum(jnp.sum(jnp.where(is_label, logits, 0.0), axis=-1, keepdims=True), "tp")
        log_norm = row_max + jnp.log(sum_exp)
        row_weight = mask_f[:, None] / mask_total
        loss_total = lax.psum(jnp.sum(row_weight * (log_norm - target)), "dp")
        soft_probs = shifted / sum_exp
        d_logits = (row_weight * jnp.where(is_label, soft_probs - 1.0, soft_probs)).astype(jnp.bfloat16)
        d_normed = lax.psum(lax.dot_general(d_logits, w_out, (((1,), (1,)), ((), ())), preferred_element_type=jnp.float32), "tp")
        d_w_out = lax.psum(lax.dot_general(normed, d_logits, (((0,), (0,)), ((), ())), preferred_element_type=jnp.float32), "dp")
        d_gain = lax.psum(jnp.sum(d_normed * x_hat, axis=0), "dp")
        value_a6 = d_normed * gain_f
        d_hidden = r_inv * (value_a6 - x_hat * jnp.mean(value_a6 * x_hat, axis=-1, keepdims=True))
        return loss_total, d_hidden.astype(jnp.bfloat16), d_w_out, d_gain

    return jax.shard_map(local_head, mesh=mesh, in_specs=(P("dp", None), P("dp"), P("dp"), P(), P(None, "tp")), out_specs=(P(), P("dp", None), P(None, "tp"), P()), check_vma=False)
```

profile of v0, /device:TPU:0, one launch (start us, length us, event | category | flops | bytes accessed | tf_op | source)
XLA Modules:
  0.0 1685.4 jit_solution(11704419113114913891)
XLA Ops:
  7.2 0.0 all-reduce.5.cloned.1.call-start
  7.2 1.3 convert_reduce_fusion
  8.5 9.2 psum.49
  17.8 1.9 convert_divide_fusion
  19.7 0.7 convert_element_type.20
  20.4 5.1 fusion.13
  25.5 0.0 copy-start.6
  25.5 78.1 %fusion.18 = (f32[2048]{0:T(1024)S(1)}, f32[2048,8000]{0,1:T(8,128)}) fusion(bf16[2048,8000]{0,1:T(8,128)(2,1)} %param.9, bf16[2048,2048]{1,0:T(8,128)(2,1)} %param.5, f32[2048]{0:T(1024)S(1)} %convert_element_type.20, f32[2048]{0:T(1024)S(1)} %add_rsqrt_fusion), kind=kOutput, calls=%fused_computation.28 | convolution fusion | flops 67142025216 | bytes 106717184 | tf_op jit(solution)/shard_map/dot_general | solution.py:20
  103.6 10.1 pmax.7
  113.7 0.0 copy-start
  113.7 0.0 copy-done.6
  113.7 0.0 copy-start.2
  113.7 21.3 %fusion.2 = (f32[2048]{0:T(1024)S(1)}, f32[2048]{0:T(1024)S(1)}) fusion(f32[2048,8000]{0,1:T(8,128)} %get-tuple-element.13, f32[2048]{0:T(1024)S(1)} %bitcast.12, s32[2048]{0:T(1024)S(1)} %broadcast_subtract_fusion), kind=kLoop, calls=%fused_computation.6 | loop fusion | flops 81915904 | bytes 65568768 | tf_op jit(solution)/shard_map/reduce_sum | solution.py:23
  135.0 14.7 all-reduce.1
  149.7 0.0 copy-start.4
  149.7 0.0 copy-done
  149.7 0.0 copy-done.2
  149.7 33.2 %fusion.1 = bf16[2048,8000]{0,1:T(8,128)(2,1)} fusion(f32[2048,8000]{0,1:T(8,128)} %get-tuple-element.13, f32[2048]{0:T(1024)S(1)} %bitcast.17, f32[2048]{0:T(1024)S(1)} %copy-done.2, s32[2048]{0:T(1024)S(1)} %broadcast_subtract_fusion, f32[2048]{0:T(1024)S(1)} %bitcast.13), kind=kLoop, calls=%fused_computation.2 | loop fusion | flops 114688000 | bytes 98336768 | tf_op jit(solution)/shard_map/convert_element_type | solution.py:30
  182.9 0.0 copy-done.4
  182.9 79.4 %fusion.19 = f32[2048,2048]{1,0:T(8,128)} fusion(bf16[2048,8000]{0,1:T(8,128)(2,1)} %fusion.1, bf16[2048,8000]{0,1:T(8,128)(2,1)} %param.9), kind=kOutput, calls=%fused_computation.29 | convolution fusion | flops 67108864000 | bytes 82313216 | tf_op jit(solution)/shard_map/dot_general | solution.py:31
  262.3 0.0 all-reduce.5.cloned.1.call-update
  262.4 0.3 all-reduce.7.cloned.1.call-start
  262.6 78.3 %fusion.14 = f32[2048,8000]{0,1:T(8,128)} fusion(bf16[2048,8000]{0,1:T(8,128)(2,1)} %fusion.1, bf16[2048,2048]{1,0:T(8,128)(2,1)} %param.5, f32[2048]{0:T(1024)S(1)} %convert_element_type.20, f32[2048]{0:T(1024)S(1)} %add_rsqrt_fusion), kind=kOutput, calls=%fused_computation.20 | convolution fusion | flops 67125641216 | bytes 106708992 | tf_op jit(solution)/shard_map/dot_general | solution.py:32
  340.9 0.0 copy-start.1
  340.9 0.0 copy-start.3
  340.9 0.0 copy-start.5
  340.9 0.0 copy-start.7
  340.9 0.0 all-reduce.7.cloned.1.call-update
  341.0 0.7 copy-done.1
  341.6 0.0 copy-done.3
  341.6 0.0 copy-done.5
  341.6 0.0 copy-done.7
  341.7 0.6 multiply_reduce_fusion
  342.3 218.7 %all-reduce.5.cloned.1.call-done = f32[2048,2048]{1,0:T(8,128)} async-done(((f32[2048,2048]{1,0:T(8,128)}), f32[2048,2048]{1,0:T(8,128)}) %all-reduce.5.cloned.1.call-update) | async-done | bytes 16777232 | tf_op jit(solution)/shard_map/psum | solution.py:31
  560.9 10.1 fusion.12
  571.0 8.2 all-reduce
  579.3 12.4 fusion.11
  591.6 1043.9 %all-reduce.7.cloned.1.call-done = f32[2048,8000]{0,1:T(8,128)} async-done(((f32[2048,8000]{0,1:T(8,128)}), f32[2048,8000]{0,1:T(8,128)}) %all-reduce.7.cloned.1.call-update) | async-done | bytes 65536016 | tf_op jit(solution)/shard_map/psum | solution.py:32
  1635.5 43.1 %copy.11 = f32[2048,8000]{0,1:T(8,128)} copy(f32[2048,8000]{0,1:T(8,128)} %all-reduce.7.cloned.1.call-done) | data formatting | bytes 131072000
  (3 shorter events, 0.0 us)
Async XLA Ops:
  7.2 553.8 %all-reduce.5.cloned.1.call-start = ((), (), s32[]{:S(2)}) async-start(), calls=%async_computation | async-start | bytes 33554432 | tf_op jit(solution)/shard_map/psum | solution.py:31
  25.5 88.2 %copy-start.6 = (s32[2048]{0:T(1024)S(1)}, s32[2048]{0:T(1024)}, u32[]{:S(2)}) copy-start(s32[2048]{0:T(1024)} %param.6) | copy-start | bytes 24580
  113.7 36.0 %copy-start = (f32[2048,1]{0,1:T(1,128)}, f32[2048,1]{0,1:T(1,128)S(1)}, u32[]{:S(2)}) copy-start(f32[2048,1]{0,1:T(1,128)S(1)} %pmax.7) | copy-start | bytes 24580
  113.7 36.0 %copy-start.2 = (f32[2048]{0:T(1024)S(1)}, f32[2048]{0:T(1024)}, u32[]{:S(2)}) copy-start(f32[2048]{0:T(1024)} %convert_divide_fusion) | copy-start | bytes 24580
  149.7 33.2 %copy-start.4 = (f32[2048,1]{0,1:T(1,128)}, f32[2048,1]{0,1:T(1,128)S(1)}, u32[]{:S(2)}) copy-start(f32[2048,1]{0,1:T(1,128)S(1)} %get-tuple-element.11) | copy-start | bytes 24580
  262.4 1373.1 %all-reduce.7.cloned.1.call-start = ((), (), s32[]{:S(2)}) async-start(), calls=%async_computation.1 | async-start | bytes 131072000 | tf_op jit(solution)/shard_map/psum | solution.py:32
  340.9 0.7 copy-start.1
  340.9 0.7 copy-start.3
  340.9 0.7 copy-start.5
  340.9 0.7 copy-start.7
Sparse Core Ops, SparseCore 0:
  262.5 298.4 all-reduce.4
  564.0 1071.4 all-reduce.6
where the time goes:
time: 1690 us
  waiting for transfers between devices  1260 us (75%)
  matrix products  236 us (14%)
  other arithmetic  86.5 us (5%)
  local copies, waits for them, and re-layouts  43.8 us (3%)
  blocking collectives  42.3 us (3%)
    psum x1, waiting for transfers between devices, local_head(): lax.psum(lax.dot_general(normed, d_logits, (((0,), (0,)), ((), ())), pref...  1040 us
    psum x1, waiting for transfers between devices, local_head(): lax.psum(lax.dot_general(d_logits, w_out, (((1,), (1,)), ((), ())), prefe...  219 us
    dot_general x1, matrix products, local_head(): lax.dot_general(d_logits, w_out, (((1,), (1,)), ((), ())), preferred_elem...  79.4 us
    dot_general x1, matrix products, local_head(): lax.dot_general(normed, d_logits, (((0,), (0,)), ((), ())), preferred_ele...  78.3 us
    dot_general x1, matrix products, local_head(): logits = jnp.dot(normed, w_out, preferred_element_type=jnp.float32)  78.1 us
    unnamed x17, local copies, waits for them, and re-layouts  43.8 us
  transfers between devices with their start and end apart: 2, of which 2 were waited for; matrix products, arithmetic and copies ran while one was open for 6% of the time, Pallas kernels for 0%

commit v1 on v0

v1 whole, which is shorter than its diff:
```python
import functools

import jax
import jax.numpy as jnp
from jax import lax
from jax.experimental import pallas as pl
from jax.experimental.pallas import tpu as pltpu
from jax.sharding import PartitionSpec as P


NORM_EPS = 1e-5

F32, BF16 = jnp.float32, jnp.bfloat16
VMEM_LIMIT = 66_000_000


def params():
    return pltpu.CompilerParams(dimension_semantics=("arbitrary",), vmem_limit_bytes=VMEM_LIMIT)


def once(shape, index):
    return pl.BlockSpec(shape, index, pipeline_mode=pl.Buffered(1))


def logits_kernel(half, strip, nt, with_target, *refs):
    *refs, zb = refs
    if with_target:
        yt_ref, w_ref, lab_ref, z_ref, m_ref, s_ref, t_ref = refs
    else:
        yt_ref, w_ref, z_ref, m_ref, s_ref = refs
    rows = yt_ref.shape[0] if nt else yt_ref.shape[1]
    j = pl.program_id(0)

    def stats(buf, lo, base, fresh):
        for c in range(0, rows, strip):
            cs = slice(c, c + strip)
            z = buf[lo:lo + half, cs].reshape(half // 8, 8, strip)
            old = m_ref[:, cs]
            if fresh is not None:
                old = jnp.where(fresh, -jnp.inf, old)
            new = jnp.maximum(old, jnp.max(z, axis=0))
            total = jnp.sum(jnp.exp(z - new), axis=0)
            keep = s_ref[:, cs] * jnp.exp(old - new)
            if fresh is not None:
                keep = jnp.where(fresh, 0.0, keep)
            m_ref[:, cs] = new
            s_ref[:, cs] = keep + total
            if with_target:
                row = lax.broadcasted_iota(jnp.int32, (half // 8, 8, strip), 0) * 8 + lax.broadcasted_iota(jnp.int32, (half // 8, 8, strip), 1)
                at = lab_ref[:, cs] - base
                hit = jnp.sum(jnp.where(row == at, z, 0.0), axis=0)
                seen = t_ref[:, cs]
                if fresh is not None:
                    seen = jnp.where(fresh, 0.0, seen)
                t_ref[:, cs] = seen + hit

    @pl.when(j == 0)
    def _():
        z_ref[:half, :] = lax.dot_general(w_ref[:half, :], yt_ref[...], (((1,), (1 if nt else 0,)), ((), ())), preferred_element_type=F32)

    @pl.when(j > 0)
    def _():
        z_ref[:half, :] = lax.dot_general(w_ref[:half, :], yt_ref[...], (((1,), (1 if nt else 0,)), ((), ())), preferred_element_type=F32)
        stats(zb, 0, (2 * j - 1) * half, None)

    zz = lax.dot_general(w_ref[half:, :], yt_ref[...], (((1,), (1 if nt else 0,)), ((), ())), preferred_element_type=F32)
    z_ref[half:, :] = zz
    zb[...] = zz
    stats(z_ref, 0, 2 * j * half, j == 0)

    @pl.when(j == pl.num_programs(0) - 1)
    def _():
        stats(zb, 0, (2 * j + 1) * half, None)


def logits(yt, wt, lab, half=400, strip=256, nt=False):
    rows, d = yt.shape if nt else yt.shape[::-1]
    cols = wt.shape[0]
    with_target = lab is not None
    fixed = lambda shape: once(shape, lambda j: (0, 0))
    stat = jax.ShapeDtypeStruct((8, rows), F32)
    n_stat = 3 if with_target else 2
    ins = [fixed(yt.shape), pl.BlockSpec((2 * half, d), lambda j: (j, 0))]
    args = [yt, wt]
    if with_target:
        ins.append(fixed((1, rows)))
        args.append(lab)
    return pl.pallas_call(
        functools.partial(logits_kernel, half, strip, nt, with_target),
        grid=(cols // (2 * half),),
        in_specs=ins,
        out_specs=[pl.BlockSpec((2 * half, rows), lambda j: (j, 0))] + [fixed((8, rows))] * n_stat,
        out_shape=[jax.ShapeDtypeStruct((cols, rows), F32)] + [stat] * n_stat,
        scratch_shapes=[pltpu.VMEM((half, rows), F32)],
        compiler_params=params(),
        cost_estimate=pl.CostEstimate(flops=2 * rows * d * cols, bytes_accessed=rows * cols * 4 + d * cols * 2, transcendentals=rows * cols),
        name="logits",
    )(*args)


def grad_of(z, lse, weight, hit):
    p = jnp.exp(z - lse)
    return (weight * jnp.where(hit, p - 1.0, p)).astype(BF16)


def dy_kernel(cols, block, chunk, z_ref, w_ref, lse_ref, wt_ref, lab_ref, g_ref, dy_ref, ga, gb):
    rows = z_ref.shape[1]
    n = rows // chunk
    j = pl.program_id(0)
    steps = pl.cdiv(cols, block)
    last = cols - (steps - 1) * block

    @pl.when(j == 0)
    def _():
        dy_ref[...] = jnp.zeros(dy_ref.shape, F32)

    def compute(width):
        def grad(r, buf):
            cs = slice(r * chunk, (r + 1) * chunk)
            v = lax.broadcasted_iota(jnp.int32, (width, chunk), 0)
            g = grad_of(z_ref[:width, cs], lse_ref[:, cs], wt_ref[:, cs], v == lab_ref[:, cs] - j * block)
            buf[:width, :] = g
            g_ref[:width, cs] = g

        def dot(r, buf):
            dy_ref[r * chunk:(r + 1) * chunk, :] += lax.dot_general(buf[:width, :], w_ref[:width, :], (((0,), (0,)), ((), ())), preferred_element_type=F32)

        bufs = (ga, gb)
        grad(0, ga)
        for r in range(n):
            if r + 1 < n:
                grad(r + 1, bufs[(r + 1) % 2])
            dot(r, bufs[r % 2])

    if last == block:
        compute(block)
    else:
        @pl.when(j < steps - 1)
        def _():
            compute(block)

        @pl.when(j == steps - 1)
        def _():
            compute(last)


def grad_and_dy(zt, wt, lse, weight, lab, block=1024, chunk=512):
    cols, rows = zt.shape
    d = wt.shape[1]
    fixed = lambda shape: once(shape, lambda j: (0, 0))
    return pl.pallas_call(
        functools.partial(dy_kernel, cols, block, chunk),
        grid=(pl.cdiv(cols, block),),
        in_specs=[pl.BlockSpec((block, rows), lambda j: (j, 0)), pl.BlockSpec((block, d), lambda j: (j, 0))] + [fixed((1, rows))] * 3,
        out_specs=[pl.BlockSpec((block, rows), lambda j: (j, 0)), fixed((rows, d))],
        out_shape=[jax.ShapeDtypeStruct((cols, rows), BF16), jax.ShapeDtypeStruct((rows, d), F32)],
        scratch_shapes=[pltpu.VMEM((block, chunk), BF16)] * 2,
        compiler_params=params(),
        cost_estimate=pl.CostEstimate(flops=2 * rows * d * cols, bytes_accessed=rows * cols * 6 + d * cols * 2, transcendentals=rows * cols),
        name="dy",
    )(zt, wt, lse, weight, lab)


def dw_kernel(first, block, has_got, half_rows, core_ref, y0_ref, y1_ref, g0_ref, z1_ref, lse_ref, wt_ref, lab_ref, *refs):
    *refs, g1 = refs
    j = pl.program_id(0)
    which = core_ref[0]
    base = which * half_rows + (first + j) * block
    v = lax.broadcasted_iota(jnp.int32, z1_ref.shape, 0)
    g1[...] = grad_of(z1_ref[...], lse_ref[...], wt_ref[...], v == lab_ref[...] - base)
    acc = jnp.dot(g0_ref[...], y0_ref[...], preferred_element_type=F32)
    if has_got:
        acc += refs[0][...]
    acc += jnp.dot(g1[...], y1_ref[...], preferred_element_type=F32)
    refs[-1][...] = acc


def dw_part(which, y0, y1, g0t, z1t, lse, weight, lab, first, blocks, got=None, block=400):
    rows, d = y0.shape
    cols = g0t.shape[0]
    per_half = cols // 2 // block
    fixed = lambda shape: once(shape, lambda j, c: (0, 0))
    part = pl.BlockSpec((block, rows), lambda j, c: (c[0] * per_half + first + j, 0))
    out = pl.BlockSpec((block, d), lambda j, c: (j, 0))
    n = blocks * block
    extra = [] if got is None else [got]
    return pl.pallas_call(
        functools.partial(dw_kernel, first, block, got is not None, cols // 2),
        grid_spec=pltpu.PrefetchScalarGridSpec(
            num_scalar_prefetch=1,
            grid=(blocks,),
            in_specs=[fixed((rows, d)), fixed((rows, d)), part, part] + [fixed((1, rows))] * 3 + [out] * len(extra),
            out_specs=out,
            scratch_shapes=[pltpu.VMEM((block, rows), BF16)],
        ),
        out_shape=jax.ShapeDtypeStruct((n, d), F32),
        compiler_params=params(),
        cost_estimate=pl.CostEstimate(flops=4 * rows * d * n, bytes_accessed=rows * n * 6 + n * d * 4 * (1 + len(extra)) + rows * d * 4, transcendentals=rows * n),
        name="dw",
    )(which, y0, y1, g0t, z1t, lse, weight, lab, *extra)


def dw_final_kernel(first, block, half_rows, n_in, core_ref, y0_ref, y1_ref, g0_ref, z1_ref, lse_ref, wt_ref, lab_ref, *refs):
    got_ref, fin_ref, big_ref, g1 = refs[0], refs[n_in], refs[n_in + 1], refs[n_in + 2]
    base = core_ref[0] * half_rows + (first + pl.program_id(0)) * block
    v = lax.broadcasted_iota(jnp.int32, z1_ref.shape, 0)
    g1[...] = grad_of(z1_ref[...], lse_ref[...], wt_ref[...], v == lab_ref[...] - base)
    acc = jnp.dot(g0_ref[...], y0_ref[...], preferred_element_type=F32)
    acc += got_ref[...]
    acc += jnp.dot(g1[...], y1_ref[...], preferred_element_type=F32)
    fin_ref[...] = acc
    big_ref[...] = acc


def dw_final(which, y0, y1, g0t, z1t, lse, weight, lab, first, blocks, got, big=None, block=400):
    rows, d = y0.shape
    cols = g0t.shape[0]
    per_half = cols // 2 // block
    fixed = lambda shape: once(shape, lambda j, c: (0, 0))
    part = lambda width: pl.BlockSpec((block, width), lambda j, c: (c[0] * per_half + first + j, 0))
    out = pl.BlockSpec((block, d), lambda j, c: (j, 0))
    n = blocks * block
    extra = [] if big is None else [big]
    n_in = 1 + len(extra)
    return pl.pallas_call(
        functools.partial(dw_final_kernel, first, block, cols // 2, n_in),
        grid_spec=pltpu.PrefetchScalarGridSpec(
            num_scalar_prefetch=1,
            grid=(blocks,),
            in_specs=[fixed((rows, d)), fixed((rows, d)), part(rows), part(rows)] + [fixed((1, rows))] * 3 + [out] + [pl.BlockSpec(memory_space=pl.ANY)] * len(extra),
            out_specs=[out, part(d)],
            scratch_shapes=[pltpu.VMEM((block, rows), BF16)],
        ),
        out_shape=[jax.ShapeDtypeStruct((n, d), F32), jax.ShapeDtypeStruct((cols, d), F32)],
        input_output_aliases={9: 1} if extra else {},
        compiler_params=params(),
        cost_estimate=pl.CostEstimate(flops=4 * rows * d * n, bytes_accessed=rows * n * 6 + n * d * 12 + rows * d * 4, transcendentals=rows * n),
        name="dw_final",
    )(which, y0, y1, g0t, z1t, lse, weight, lab, got, *extra)


def place_kernel(which_ref, src_ref, big_in, big_ref):
    big_ref[...] = src_ref[...]


def place(which, src, big, first, block=400):
    n, d = src.shape
    cols = big.shape[0]
    per_half = cols // 2 // block
    return pl.pallas_call(
        place_kernel,
        grid_spec=pltpu.PrefetchScalarGridSpec(
            num_scalar_prefetch=1,
            grid=(n // block,),
            in_specs=[pl.BlockSpec((block, d), lambda j, c: (j, 0)), pl.BlockSpec(memory_space=pl.ANY)],
            out_specs=pl.BlockSpec((block, d), lambda j, c: (c[0] * per_half + first + j, 0)),
        ),
        out_shape=jax.ShapeDtypeStruct(big.shape, F32),
        input_output_aliases={2: 0},
        compiler_params=params(),
        cost_estimate=pl.CostEstimate(flops=n * d * 100, bytes_accessed=n * d * 8, transcendentals=0),
        name="place",
    )(which, src, big)


def tail_kernel(dy_ref, h_ref, gain_ref, dh_ref, dg_ref):
    @pl.when(pl.program_id(0) == 0)
    def _():
        dg_ref[...] = jnp.zeros(dg_ref.shape, F32)

    x = h_ref[...].astype(F32)
    r = lax.rsqrt(jnp.mean(x * x, axis=-1, keepdims=True) + NORM_EPS)
    x = x * r
    dy = dy_ref[...]
    u = dy * gain_ref[...]
    dh_ref[...] = (r * (u - x * jnp.mean(u * x, axis=-1, keepdims=True))).astype(BF16)
    n, d = x.shape
    dg_ref[...] += jnp.sum((dy * x).reshape(n // 8, 8, d), axis=0)


def tail(dy, hidden, gain, block=256):
    rows, d = dy.shape
    row = lambda: pl.BlockSpec((block, d), lambda i: (i, 0))
    return pl.pallas_call(
        tail_kernel,
        grid=(rows // block,),
        in_specs=[row(), row(), once((1, d), lambda i: (0, 0))],
        out_specs=[row(), once((8, d), lambda i: (0, 0))],
        out_shape=[jax.ShapeDtypeStruct((rows, d), BF16), jax.ShapeDtypeStruct((8, d), F32)],
        compiler_params=params(),
        cost_estimate=pl.CostEstimate(flops=rows * d * 100, bytes_accessed=rows * d * 8, transcendentals=rows),
        name="tail",
    )(dy, hidden, gain)


def solution(mesh):
    n_tp = mesh.shape["tp"]
    n_dp = mesh.shape["dp"]
    half = n_dp // 2
    swap_x = [(i, (i + half) % n_dp) for i in range(n_dp)]
    swap_core = [(i, i ^ 1) for i in range(n_dp)]
    barrier = lax.optimization_barrier

    def dp_sum(v):
        total = v
        for k in range(1, n_dp):
            total = total + lax.ppermute(v, "dp", [(i, i ^ k) for i in range(n_dp)])
        return total

    def local_head(hidden, labels, loss_mask, norm_gain, w_out):
        return body(hidden, labels, loss_mask, norm_gain, w_out.T)

    def body(hidden, labels, loss_mask, norm_gain, wt):
        rows, d = hidden.shape
        cols = wt.shape[0]
        tp = lax.axis_index("tp")
        core = (lax.axis_index("dp") % 2).astype(jnp.int32)
        own_id = core.reshape(1)
        other_id = 1 - own_id
        start = tp * cols

        mask_f = loss_mask.astype(F32)
        gain_f = norm_gain.astype(F32)

        def normed(h):
            h = h.astype(F32)
            return h * lax.rsqrt(jnp.mean(h * h, axis=-1, keepdims=True) + NORM_EPS)

        direct = rows // 4
        quarter = (rows - direct) // n_tp
        mine = normed(lax.dynamic_slice_in_dim(hidden, direct + tp * quarter, quarter, 0))
        straight = normed(hidden[:direct])
        count = jnp.full((8, 128), jnp.sum(mask_f))
        small = jnp.stack([labels, loss_mask])
        mine, straight, small, count, hidden = barrier((mine, straight, small, count, hidden))
        far_q = lax.ppermute(mine, "dp", swap_x)
        far_s = lax.ppermute(straight, "dp", swap_x)
        small_far = lax.ppermute(small, "dp", swap_x)
        mask_total = dp_sum(count)[0, 0]
        far_g = lax.all_gather(far_q, "tp", axis=0, tiled=True)
        y0 = barrier((normed(hidden) * gain_f).astype(BF16))

        def merge(m8, s8, t8):
            m = jnp.max(m8, axis=0)
            s = jnp.sum(s8 * jnp.exp(m8 - m), axis=0)
            stats = [m, s] if t8 is None else [m, s, jnp.sum(t8, axis=0)]
            stats = lax.all_gather(jnp.stack(stats), "tp")
            m_all = jnp.max(stats[:, 0], axis=0)
            s_all = jnp.sum(stats[:, 1] * jnp.exp(stats[:, 0] - m_all), axis=0)
            return m_all + jnp.log(s_all), None if t8 is None else jnp.sum(stats[:, 2], axis=0)

        lab0 = (labels - start)[None]
        z0, m8, s8, t8 = logits(y0, wt, lab0, nt=True)
        lse0, t0 = merge(m8, s8, t8)
        w0 = mask_f / mask_total
        g0, dy = grad_and_dy(z0, wt, lse0[None], w0[None], lab0, chunk=1024)
        d_normed = lax.psum(dy, "tp")

        far_s, far_g, small_far, gain_1, g0, _ = barrier((far_s, far_g, small_far, gain_f, g0, dy))
        y1 = (jnp.concatenate([far_s, far_g], 0) * gain_1).astype(BF16)
        z1, m8, s8 = logits(y1, wt, None, nt=True)
        lse1, _ = merge(m8, s8, None)
        lab1 = (small_far[0] - start)[None]
        w1 = small_far[1].astype(F32) / mask_total
        args = (y0, y1, g0, z1, lse1[None], w1[None], lab1)
        n = cols // 800 // 2
        pa = dw_part(other_id, *args, 0, n)
        got_a = lax.ppermute(pa, "dp", swap_core)
        pb = dw_part(other_id, *args, n, n)
        got_b = lax.ppermute(pb, "dp", swap_core)
        got_a, pb = barrier((got_a, pb))
        fa, big = dw_final(own_id, *args, 0, n, got_a)
        peer_a = lax.ppermute(fa, "dp", swap_core)
        fb, big = dw_final(own_id, *args, n, n, got_b, big)
        peer_b = lax.ppermute(fb, "dp", swap_core)
        big = place(other_id, peer_a, big, 0)
        d_normed, big = barrier((d_normed, big))
        d_hidden, dg8 = tail(d_normed, hidden, gain_f[None])
        big = place(other_id, peer_b, big, n)

        loss_part = jnp.sum(w0 * (lse0 - t0))
        sums = lax.psum(jnp.concatenate([jnp.sum(dg8, axis=0), jnp.full((128,), loss_part)]), "dp")
        return sums[d], d_hidden, big.T, sums[:d]

    return jax.shard_map(local_head, mesh=mesh, in_specs=(P("dp", None), P("dp"), P("dp"), P(), P(None, "tp")), out_specs=(P(), P("dp", None), P(None, "tp"), P()), check_vma=False)
```

time: 1690 us -> 872 us (0.52)
  waiting for transfers between devices: 1260 us -> 257 us
  Pallas kernels: 0 us -> 507 us
  matrix products: 236 us -> 0 us
  other arithmetic: 86.5 us -> 47 us
  local copies, waits for them, and re-layouts: 43.8 us -> 4.58 us
    psum x2 -> x1, waiting for transfers between devices: 1260 us -> 189 us  [body(): d_normed = lax.psum(dy, 'tp')]
    pallas_call x0 -> x10, Pallas kernels: none -> 507 us  [the longest x2 187 us: logits(): pl.pallas_call(functools.partial(logits_kernel, half, strip, nt, with_tar...]
    dot_general x3 -> x0, matrix products: 236 us -> none  [the longest x1 79.4 us: local_head(): lax.dot_general(d_logits, w_out, (((1,), (1,)), ((), ())), preferred_elem...]
    ppermute x0 -> x10, waiting for transfers between devices: none -> 68.1 us  [the longest x1 68.1 us: body(): far_q = lax.ppermute(mine, 'dp', swap_x)]
    unnamed x17 -> x10, local copies, waits for them, and re-layouts: 43.8 us -> 1.69 us
    convert_element_type x3, other arithmetic: 46.2 us -> 19.6 us  [the longest x1 9.91 us: body(): y0 = barrier((normed(hidden) * gain_f).astype(BF16))]
    reduce_sum x5 -> x11, other arithmetic: 38.4 us -> 16.8 us  [the longest x3 9.98 us: normed(): return h * lax.rsqrt(jnp.mean(h * h, axis=-1, keepdims=True) + NORM_EPS)]
    psum x3 -> x1, blocking collectives: 32.2 us -> 10.7 us  [body(): lax.psum(jnp.concatenate([jnp.sum(dg8, axis=0), jnp.full((128,), loss_par...]
  transfers between devices with their start and end apart: 2 -> 12, of which waited for: 2 -> 2; matrix products, arithmetic and copies ran while one was open for 6% -> 3% of each run, Pallas kernels for 0% -> 42%
where the time goes in v1:
time: 872 us; the launch traced here: 866 us
  Pallas kernels  507 us (58%)
  waiting for transfers between devices  257 us (29%)
  other arithmetic  47 us (5%)
  blocking collectives  27.7 us (3%)
  between operations  14.7 us (2%)
    psum x1, waiting for transfers between devices, body(): d_normed = lax.psum(dy, 'tp')  189 us
    pallas_call x2, Pallas kernels, logits(): pl.pallas_call(functools.partial(logits_kernel, half, strip, nt, with_tar...  187 us
    pallas_call x2, Pallas kernels, dw_final(): pl.pallas_call(functools.partial(dw_final_kernel, first, block, cols // 2...  97.3 us
    pallas_call x1, Pallas kernels, grad_and_dy(): pl.pallas_call(functools.partial(dy_kernel, cols, block, chunk), grid=(pl...  91.1 us
    pallas_call x2, Pallas kernels, dw_part(): pl.pallas_call(functools.partial(dw_kernel, first, block, got is not None...  88.9 us
    ppermute x1, waiting for transfers between devices, body(): far_q = lax.ppermute(mine, 'dp', swap_x)  68.1 us
    pallas_call x2, Pallas kernels, place(): pl.pallas_call(place_kernel, grid_spec=pltpu.PrefetchScalarGridSpec(num_s...  26.5 us
  transfers between devices with their start and end apart: 12, of which 2 were waited for; matrix products, arithmetic and copies ran while one was open for 3% of the time, Pallas kernels for 42%

profile of v1, /device:TPU:0, one launch (start us, length us, event | category | flops | bytes accessed | tf_op | source)
XLA Modules:
  0.0 866.1 jit_solution(4678722670028540666)
XLA Ops:
  7.2 0.0 all-gather.6.cloned.1.call-start
  7.2 1.3 convert_reduce_fusion
  8.6 2.1 fusion.4
  10.6 1.8 fusion.5
  12.4 1.7 convert_multiply_fusion.4
  14.1 3.9 convert_multiply_fusion.2
  18.0 0.6 broadcast_in_dim.8
  18.7 3.2 collective-permute-start.4
  21.9 68.1 %collective-permute-done.4 = f32[384,2048]{1,0:T(8,128)S(1)} collective-permute-done((f32[384,2048]{1,0:T(8,128)S(1)}, f32[384,2048]{1,0:T(8,128)S(1)}, u32[]{:S(2)}, u32[]{:S(2)}) %collective-permute-start.4) | collective-permute-done | bytes 3145760 | tf_op jit(solution)/shard_map/ppermute | solution.py:336
  90.0 1.7 copy-done
  91.7 0.0 all-gather.6.cloned.1.call-update
  91.7 0.0 all-reduce.3.cloned.1.call-start
  91.8 0.4 collective-permute-start.2
  92.1 1.5 collective-permute-start.1
  93.6 0.1 collective-permute-start
  93.7 1.7 collective-permute-start.5
  95.4 0.3 collective-permute-start.3
  95.7 6.1 fusion
  101.8 9.9 %fusion.2.refs_0_.y0_ref = bf16[2048,2048]{1,0:T(8,128)(2,1)} fusion(bf16[2048,2048]{1,0:T(8,128)(2,1)} %h_ref, f32[2048]{0:T(1024)S(1)} %convert_element_type.29, f32[2048]{0:T(1024)S(1)} %add_rsqrt_fusion), kind=kLoop, calls=%fused_computation.4 | loop fusion | flops 16777216 | bytes 16793600 | tf_op jit(solution)/shard_map/convert_element_type | solution.py:341
  111.7 0.6 broadcast_subtract_fusion
  112.3 98.6 %logits.2 = (f32[8000,2048]{1,0:T(8,128)}, f32[8,2048]{1,0:T(8,128)}, f32[8,2048]{1,0:T(8,128)}, f32[8,2048]{1,0:T(8,128)}) custom-call(bf16[2048,2048]{1,0:T(8,128)(2,1)} %fusion.2.refs_0_.y0_ref, bf16[8000,2048]{1,0:T(8,128)(2,1)} %bitcast.62, s32[1,2048]{1,0:T(1,128)} %bitcast.60), custom_call_target="tpu_custom_call" | custom-call | flops 67108864000 | bytes 98304000 | tf_op jit(solution)/shard_map/logits/pallas_call | solution.py:88
  210.9 0.9 reduce_max.36
  211.7 0.9 reduce_sum.113
  212.6 0.9 multiply_reduce_fusion.1
  213.5 8.7 %all-gather.2 = f32[4,3,2048]{2,1,0:T(4,128)S(1)} all-gather(f32[1,3,2048]{2,1,0:T(4,128)S(1)} %maximum_bitcast_fusion), channel_id=2, replica_groups=mesh['tp'=4,'dp'=4] {'tp'}, dimensions={0}, use_global_device_ids=true | all-gather | bytes 122880 | tf_op jit(solution)/shard_map/all_gather | solution.py:347
  222.3 0.1 fusion.13
  222.5 0.0 collective-permute-done.2
  222.5 0.0 collective-permute-done.1
  222.5 0.0 collective-permute-done
  222.5 0.5 slice.38
  223.0 1.9 multiply_reduce_fusion.2
  224.9 91.1 %dy.1 = (bf16[8000,2048]{1,0:T(8,128)(2,1)}, f32[2048,2048]{1,0:T(8,128)}) custom-call(f32[8000,2048]{1,0:T(8,128)} %get-tuple-element.33.z_ref, bf16[8000,2048]{1,0:T(8,128)(2,1)} %bitcast.63, f32[1,2048]{1,0:T(1,128)} %bitcast.59, f32[1,2048]{1,0:T(1,128)} %bitcast.58, s32[1,2048]{1,0:T(1,128)} %bitcast.61), custom_call_target="tpu_custom_call" | custom-call | flops 67108864000 | bytes 131072000 | tf_op jit(solution)/shard_map/dy/pallas_call | solution.py:151
  316.0 0.0 collective-permute-done.5
  316.0 0.0 collective-permute-done.3
  316.0 0.0 all-gather.6.cloned.1.call-done
  316.1 0.6 slice_subtract_fusion.lab_ref
  316.7 1.3 convert_divide_fusion.wt_ref
  317.9 9.7 %fusion.3.refs_0_.y1_ref = bf16[2048,2048]{1,0:T(8,128)(2,1)} fusion(f32[1536,2048]{1,0:T(8,128)} %all-gather.6.cloned.1.call-done, f32[512,2048]{1,0:T(8,128)} %collective-permute-done.3, f32[2048]{0:T(1024)S(1)} %convert_element_type.29), kind=kLoop, calls=%fused_computation.6 | loop fusion | flops 12582912 | bytes 25174016 | tf_op jit(solution)/shard_map/convert_element_type | solution.py:360
  327.6 88.5 %logits.3 = (f32[8000,2048]{1,0:T(8,128)}, f32[8,2048]{1,0:T(8,128)}, f32[8,2048]{1,0:T(8,128)}) custom-call(bf16[2048,2048]{1,0:T(8,128)(2,1)} %fusion.3.refs_0_.y1_ref, bf16[8000,2048]{1,0:T(8,128)(2,1)} %bitcast.64), custom_call_target="tpu_custom_call" | custom-call | flops 67108864000 | bytes 98304000 | tf_op jit(solution)/shard_map/logits/pallas_call | solution.py:88
  416.1 0.9 reduce_max.38
  417.0 0.9 multiply_reduce_fusion
  417.9 8.3 all-gather.3
  426.1 0.1 fusion.14
  426.3 0.6 log_add_fusion
  426.9 44.5 %dw.2 = f32[2000,2048]{1,0:T(8,128)} custom-call(s32[1]{0:T(128)S(6)} %sub.57.core_ref.which_ref, bf16[2048,2048]{1,0:T(8,128)(2,1)} %fusion.2.refs_0_.y0_ref, bf16[2048,2048]{1,0:T(8,128)(2,1)} %fusion.3.refs_0_.y1_ref, bf16[8000,2048]{1,0:T(8,128)(2,1)} %get-tuple-element.46.g0_ref, f32[8000,2048]{1,0:T(8,128)} %get-tuple-element.47.z1_ref, ...), custom_call_target="tpu_custom_call" | custom-call | flops 33554432000 | bytes 57737216 | tf_op jit(solution)/shard_map/dw/pallas_call | solution.py:187
  471.4 0.0 collective-permute-start.6
  471.4 44.4 %dw.3 = f32[2000,2048]{1,0:T(8,128)} custom-call(s32[1]{0:T(128)S(6)} %sub.57.core_ref.which_ref, bf16[2048,2048]{1,0:T(8,128)(2,1)} %fusion.2.refs_0_.y0_ref, bf16[2048,2048]{1,0:T(8,128)(2,1)} %fusion.3.refs_0_.y1_ref, bf16[8000,2048]{1,0:T(8,128)(2,1)} %get-tuple-element.46.g0_ref, f32[8000,2048]{1,0:T(8,128)} %get-tuple-element.47.z1_ref, ...), custom_call_target="tpu_custom_call" | custom-call | flops 33554432000 | bytes 57737216 | tf_op jit(solution)/shard_map/dw/pallas_call | solution.py:187
  515.7 0.5 collective-permute-start.8
  516.2 0.0 all-reduce.3.cloned.1.call-update
  516.3 0.0 collective-permute-done.6.refs_0_
  516.3 48.9 %dw_final.2 = (f32[2000,2048]{1,0:T(8,128)}, f32[8000,2048]{1,0:T(8,128)}) custom-call(s32[1]{0:T(128)} %bitcast.12.core_ref, bf16[2048,2048]{1,0:T(8,128)(2,1)} %fusion.2.refs_0_.y0_ref, bf16[2048,2048]{1,0:T(8,128)(2,1)} %fusion.3.refs_0_.y1_ref, bf16[8000,2048]{1,0:T(8,128)(2,1)} %get-tuple-element.46.g0_ref, f32[8000,2048]{1,0:T(8,128)} %get-tuple-element.47.z1_ref, ...), custom_call_target="tpu_custom_call" | custom-call | flops 33554432000 | bytes 90505216 | tf_op jit(solution)/shard_map/dw_final/pallas_call | solution.py:225
  565.2 0.0 collective-permute-start.7
  565.2 48.4 %dw_final.3 = (f32[2000,2048]{1,0:T(8,128)}, f32[8000,2048]{1,0:T(8,128)}) custom-call(s32[1]{0:T(128)} %bitcast.12.core_ref, bf16[2048,2048]{1,0:T(8,128)(2,1)} %fusion.2.refs_0_.y0_ref, bf16[2048,2048]{1,0:T(8,128)(2,1)} %fusion.3.refs_0_.y1_ref, bf16[8000,2048]{1,0:T(8,128)(2,1)} %get-tuple-element.46.g0_ref, ...), custom_call_target="tpu_custom_call", output_to_operand_aliasing={{1}: (9, {})} | custom-call | flops 33554432000 | bytes 90505216 | tf_op jit(solution)/shard_map/dw_final/pallas_call | solution.py:225
  613.6 0.5 collective-permute-start.9
  614.1 0.0 collective-permute-done.7.src_ref
  614.1 13.3 %place.2.big_in = f32[8000,2048]{1,0:T(8,128)} custom-call(s32[1]{0:T(128)S(6)} %sub.57.core_ref.which_ref, f32[2000,2048]{1,0:T(8,128)} %collective-permute-done.7.src_ref, f32[8000,2048]{1,0:T(8,128)} %get-tuple-element.54.big_in), custom_call_target="tpu_custom_call", output_to_operand_aliasing={{}: (2, {})} | custom-call | flops 409600000 | bytes 32768000 | tf_op jit(solution)/shard_map/place/pallas_call | solution.py:250
  627.4 188.9 %all-reduce.3.cloned.1.call-done.dy_ref = f32[2048,2048]{1,0:T(8,128)} async-done(((f32[2048,2048]{1,0:T(8,128)}), f32[2048,2048]{1,0:T(8,128)}) %all-reduce.3.cloned.1.call-update) | async-done | bytes 16777232 | tf_op jit(solution)/shard_map/psum | solution.py:357
  816.3 16.1 %tail.1 = (bf16[2048,2048]{1,0:T(8,128)(2,1)}, f32[8,2048]{1,0:T(8,128)}) custom-call(f32[2048,2048]{1,0:T(8,128)} %all-reduce.3.cloned.1.call-done.dy_ref, bf16[2048,2048]{1,0:T(8,128)(2,1)} %h_ref, f32[1,2048]{1,0:T(1,128)} %bitcast.50), custom_call_target="tpu_custom_call" | custom-call | flops 419430400 | bytes 33554432 | tf_op jit(solution)/shard_map/tail/pallas_call | solution.py:284
  832.4 0.9 reduce_sum.117
  833.3 0.6 concatenate.7
  833.9 10.7 %psum.15 = f32[2176]{0:T(1024)S(1)} all-reduce(f32[2176]{0:T(1024)S(1)} %concatenate.7), channel_id=1, replica_groups=mesh['tp'=4,'dp'=4] {'dp'}, use_global_device_ids=true, to_apply=%region_17.18 | all-reduce | flops 2176 | bytes 17408 | tf_op jit(solution)/shard_map/psum | solution.py:382
  844.6 0.5 slice.51
  845.1 0.6 slice.52
  845.7 13.2 %place.3 = f32[8000,2048]{1,0:T(8,128)} custom-call(s32[1]{0:T(128)S(6)} %sub.57.core_ref.which_ref, f32[2000,2048]{1,0:T(8,128)} %collective-permute-done.9.src_ref, f32[8000,2048]{1,0:T(8,128)} %place.2.big_in), custom_call_target="tpu_custom_call", output_to_operand_aliasing={{}: (2, {})} | custom-call | flops 409600000 | bytes 32768000 | tf_op jit(solution)/shard_map/place/pallas_call | solution.py:250
  (21 shorter events, 0.2 us)
Async XLA Ops:
  7.2 10.8 %copy-start.2 = (s32[2048]{0:T(1024)S(1)}, s32[2048]{0:T(1024)}, u32[]{:S(2)}) copy-start(s32[2048]{0:T(1024)} %param.7) | copy-start | bytes 24580
  7.2 10.8 %copy-start.3 = (s32[2048]{0:T(1024)S(1)}, s32[2048]{0:T(1024)}, u32[]{:S(2)}) copy-start(s32[2048]{0:T(1024)} %param.6) | copy-start | bytes 24580
  7.2 88.5 %copy-start.4 = (bf16[2048]{0:T(1024)(128)(2,1)S(1)}, bf16[2048]{0:T(1024)(128)(2,1)}, u32[]{:S(2)}) copy-start(bf16[2048]{0:T(1024)(128)(2,1)} %param.8) | copy-start | bytes 12292
  7.2 308.9 %all-gather.6.cloned.1.call-start = ((), (), s32[]{:S(2)}) async-start(), calls=%async_computation.1 | async-start | bytes 15728640 | tf_op jit(solution)/shard_map/all_gather | solution.py:340
  18.7 71.3 %collective-permute-start.4 = (f32[384,2048]{1,0:T(8,128)S(1)}, f32[384,2048]{1,0:T(8,128)S(1)}, u32[]{:S(2)}, u32[]{:S(2)}) collective-permute-start(f32[384,2048]{1,0:T(8,128)S(1)} %convert_multiply_fusion.4), channel_id=1, source_target_pairs={{0,2},{1,3},{2,0},{3,1},{4,6},{5,7},{6,4},{7,5},{8,10},{9,11},{10,... | collective-permute-start | bytes 9437192 | tf_op jit(solution)/shard_map/ppermute | solution.py:336
  90.0 1.7 copy-start
  91.7 724.6 %all-reduce.3.cloned.1.call-start = ((), (), s32[]{:S(2)}) async-start(), calls=%async_computation | async-start | bytes 33554432 | tf_op jit(solution)/shard_map/psum | solution.py:357
  91.8 130.7 %collective-permute-start.2 = (f32[8,128]{1,0:T(8,128)S(1)}, f32[8,128]{1,0:T(8,128)S(1)}, u32[]{:S(2)}, u32[]{:S(2)}) collective-permute-start(f32[8,128]{1,0:T(8,128)S(1)} %broadcast_in_dim.8), channel_id=1, source_target_pairs={{0,3},{1,2},{2,1},{3,0},{4,7},{5,6},{6,5},{7,4},{8,11},{9,10},{10,... | collective-permute-start | bytes 12296 | tf_op jit(solution)/shard_map/ppermute | solution.py:307
  92.1 130.4 %collective-permute-start.1 = (f32[8,128]{1,0:T(8,128)S(1)}, f32[8,128]{1,0:T(8,128)S(1)}, u32[]{:S(2)}, u32[]{:S(2)}) collective-permute-start(f32[8,128]{1,0:T(8,128)S(1)} %broadcast_in_dim.8), channel_id=1, source_target_pairs={{0,2},{1,3},{2,0},{3,1},{4,6},{5,7},{6,4},{7,5},{8,10},{9,11},{10,... | collective-permute-start | bytes 12296 | tf_op jit(solution)/shard_map/ppermute | solution.py:307
  93.6 128.9 %collective-permute-start = (f32[8,128]{1,0:T(8,128)S(1)}, f32[8,128]{1,0:T(8,128)S(1)}, u32[]{:S(2)}, u32[]{:S(2)}) collective-permute-start(f32[8,128]{1,0:T(8,128)S(1)} %broadcast_in_dim.8), channel_id=1, source_target_pairs={{0,1},{1,0},{2,3},{3,2},{4,5},{5,4},{6,7},{7,6},{8,9},{9,8},{10,11... | collective-permute-start | bytes 12296 | tf_op jit(solution)/shard_map/ppermute | solution.py:307
  93.7 222.4 %collective-permute-start.5 = (s32[2,2048]{1,0:T(2,128)S(1)}, s32[2,2048]{1,0:T(2,128)S(1)}, u32[]{:S(2)}, u32[]{:S(2)}) collective-permute-start(s32[2,2048]{1,0:T(2,128)S(1)} %pad_add_fusion), channel_id=1, source_target_pairs={{0,2},{1,3},{2,0},{3,1},{4,6},{5,7},{6,4},{7,5},{8,10},{9,11},{10,... | collective-permute-start | bytes 49160 | tf_op jit(solution)/shard_map/ppermute | solution.py:338
  95.4 220.6 %collective-permute-start.3 = (f32[512,2048]{1,0:T(8,128)}, f32[512,2048]{1,0:T(8,128)}, u32[]{:S(2)}, u32[]{:S(2)}) collective-permute-start(f32[512,2048]{1,0:T(8,128)} %convert_multiply_fusion.2), channel_id=1, source_target_pairs={{0,2},{1,3},{2,0},{3,1},{4,6},{5,7},{6,4},{7,5},{8,10},{9,11},{10,... | collective-permute-start | bytes 12582920 | tf_op jit(solution)/shard_map/ppermute | solution.py:337
  95.7 222.3 %copy-start.1 = (f32[2048]{0:T(1024)}, f32[2048]{0:T(1024)S(1)}, u32[]{:S(2)}) copy-start(f32[2048]{0:T(1024)S(1)} %convert_element_type.29) | copy-start | bytes 24580
  471.4 44.9 %collective-permute-start.6 = (f32[2000,2048]{1,0:T(8,128)}, f32[2000,2048]{1,0:T(8,128)}, u32[]{:S(2)}, u32[]{:S(2)}) collective-permute-start(f32[2000,2048]{1,0:T(8,128)} %dw.2), channel_id=1, source_target_pairs={{0,1},{1,0},{2,3},{3,2},{4,5},{5,4},{6,7},{7,6},{8,9},{9,8},{10,11... | collective-permute-start | bytes 49152008 | tf_op jit(solution)/shard_map/ppermute | solution.py:368
  515.7 49.5 %collective-permute-start.8 = (f32[2000,2048]{1,0:T(8,128)}, f32[2000,2048]{1,0:T(8,128)}, u32[]{:S(2)}, u32[]{:S(2)}) collective-permute-start(f32[2000,2048]{1,0:T(8,128)} %dw.3), channel_id=1, source_target_pairs={{0,1},{1,0},{2,3},{3,2},{4,5},{5,4},{6,7},{7,6},{8,9},{9,8},{10,11... | collective-permute-start | bytes 49152008 | tf_op jit(solution)/shard_map/ppermute | solution.py:370
  565.2 48.9 %collective-permute-start.7 = (f32[2000,2048]{1,0:T(8,128)}, f32[2000,2048]{1,0:T(8,128)}, u32[]{:S(2)}, u32[]{:S(2)}) collective-permute-start(f32[2000,2048]{1,0:T(8,128)} %get-tuple-element.52), channel_id=1, source_target_pairs={{0,1},{1,0},{2,3},{3,2},{4,5},{5,4},{6,7},{7,6},{8,9},{9,8},{10,11... | collective-permute-start | bytes 49152008 | tf_op jit(solution)/shard_map/ppermute | solution.py:373
  613.6 232.1 %collective-permute-start.9 = (f32[2000,2048]{1,0:T(8,128)}, f32[2000,2048]{1,0:T(8,128)}, u32[]{:S(2)}, u32[]{:S(2)}) collective-permute-start(f32[2000,2048]{1,0:T(8,128)} %get-tuple-element.58), channel_id=1, source_target_pairs={{0,1},{1,0},{2,3},{3,2},{4,5},{5,4},{6,7},{7,6},{8,9},{9,8},{10,11... | collective-permute-start | bytes 49152008 | tf_op jit(solution)/shard_map/ppermute | solution.py:375
Sparse Core Ops, SparseCore 0:
  91.8 119.9 all-gather.5
  516.4 299.8 all-reduce.2
